TPU v7x, 32 devices: a whole 2x2x4 slice. The times are simulated.
32 devices in a mesh: groups: 2 (over y), ctx: 4 (over z), head: 2 (over x), rep: 2 (over core).
Axes of the slice: x: 2, y: 2, z: 4, core: 2. Of those that a mesh axis runs over, the one named last changes fastest.
Arguments:
- queries: bfloat16 [2048, 4096], P(('groups', 'ctx'), ('head', 'rep')), parts along dimension 0, may hold values from -24 to 24
- keys: bfloat16 [2048, 1024], P(('groups', 'ctx'), ('head', 'rep')), parts along dimension 0, may hold values from -6 to 6
- values: bfloat16 [2048, 1024], P(('groups', 'ctx'), ('head', 'rep')), parts along dimension 0, may hold values from -6 to 6
- span_order: int32 [8], replicated, may hold values from 0 to 7, as said below
Outputs:
- attended: bfloat16 [2048, 4096], P(('groups', 'ctx'), ('head', 'rep')), parts along dimension 0
There are 2 independent parts, one for each index of `groups`. A program takes and returns all parts, laid end to end along the dimension named above; an argument that names none is the same for every part. Nothing has to cross between parts.
Inputs may be any that keep to these rules, and one draw needn't show every extreme that they name: `span_order`: A permutation of the spans in which entries 2 d and 2 d + 1 are c and 7 - c for some c.
All inputs are finite; a program needn't handle non-finite values.
Results may differ from a plain program's by a relative error of at most 0.0047.
Values may be sent and summed in bfloat16 or wider, within the bound.
A program may use at most 64 MiB of HBM per device.

v0:
```python
import math
import jax
import jax.numpy as jnp
from jax import lax
from jax.sharding import PartitionSpec as P

HEAD_SIZE = 128
masked_score = -1e30


def lookup_positions(span_order, first_row, row_count, span_rows):
    row_ids = first_row + jnp.arange(row_count, dtype=jnp.int32)
    span_ids = row_ids // span_rows
    span_table = jnp.arange(span_order.shape[0], dtype=jnp.int32)
    span_starts = jnp.sum(
        jnp.where(span_ids[:, None] == span_table[None, :], span_order[None, :], 0), axis=1
    )
    return span_starts * span_rows + row_ids % span_rows


def source_partials(query_block, query_pos, key_group, value_group, key_pos, head_dim):
    score_scale = 1.0 / math.sqrt(head_dim)
    scores = (
        jnp.einsum("rhgd,cshd->crhgs", query_block, key_group, preferred_element_type=jnp.float32)
        * score_scale
    )
    allowed = (key_pos[:, None, :] <= query_pos[None, :, None])[:, :, None, None, :]
    masked = jnp.where(allowed, scores, masked_score)
    row_top = jnp.max(masked, axis=-1)
    weights = jnp.where(allowed, jnp.exp(masked - row_top[..., None]), 0.0)
    row_total = jnp.sum(weights, axis=-1)
    numerator = jnp.einsum(
        "crhgs,cshd->crhgd",
        weights.astype(jnp.bfloat16),
        value_group,
        preferred_element_type=jnp.float32,
    )
    partial_value = (numerator / jnp.maximum(row_total, 1.0)[..., None]).astype(jnp.bfloat16)
    return (partial_value, row_top, row_total)


def absorb(running, partial_value, row_top, row_total):
    run_top, run_total, run_sum = running
    new_top = jnp.maximum(run_top, row_top)
    rescale = jnp.exp(run_top - new_top)
    source_weight = row_total * jnp.exp(row_top - new_top)
    return (
        new_top,
        run_total * rescale + source_weight,
        run_sum * rescale[..., None] + source_weight[..., None] * partial_value.astype(jnp.float32),
    )


def shards(queries, keys, values, span_order):
    rows_here = queries.shape[0]
    span_rows = rows_here // 2
    head_dim = HEAD_SIZE
    kv_heads = keys.shape[1] // head_dim
    common_values = queries.shape[1] // keys.shape[1]
    my_index = lax.axis_index("ctx")
    own_pos = lookup_positions(span_order, my_index * rows_here, rows_here, span_rows)
    q_local = queries.reshape(rows_here, kv_heads, common_values, head_dim)
    initial = (
        jnp.full((rows_here, kv_heads, common_values), masked_score, jnp.float32),
        jnp.zeros((rows_here, kv_heads, common_values), jnp.float32),
        jnp.zeros((rows_here, kv_heads, common_values, head_dim), jnp.float32),
    )
    running = initial
    k_piece = lax.all_gather(keys, "ctx", axis=0, tiled=True)
    v_piece = lax.all_gather(values, "ctx", axis=0, tiled=True)
    shard_count = k_piece.shape[0] // rows_here
    per_turn = 2
    turn_count = shard_count // per_turn
    k_pos = lookup_positions(span_order, jnp.int32(0), k_piece.shape[0], span_rows)
    k_steps = k_piece.reshape(turn_count, per_turn, rows_here, kv_heads, head_dim)
    v_steps = v_piece.reshape(turn_count, per_turn, rows_here, kv_heads, head_dim)
    p_steps = k_pos.reshape(turn_count, per_turn, rows_here)

    def one_turn(carried, inputs_now):
        partial_value, row_top, row_total = source_partials(
            q_local, own_pos, inputs_now[0], inputs_now[1], inputs_now[2], head_dim
        )
        for member in range(per_turn):
            carried = absorb(carried, partial_value[member], row_top[member], row_total[member])
        return (carried, None)

    running, unused = lax.scan(one_turn, running, (k_steps, v_steps, p_steps))
    merged = running[2] / running[1][..., None]
    return merged.reshape(rows_here, kv_heads * common_values * head_dim).astype(jnp.bfloat16)


def solution(mesh):
    return jax.shard_map(
        shards,
        mesh=mesh,
        in_specs=(
            P(("groups", "ctx"), ("head", "rep")),
            P(("groups", "ctx"), ("head", "rep")),
            P(("groups", "ctx"), ("head", "rep")),
            P(),
        ),
        out_specs=P(("groups", "ctx"), ("head", "rep")),
        check_vma=False,
    )
```

profile of v0, /device:TPU:0, one launch (start us, length us, event | category | flops | bytes accessed | tf_op | source)
XLA Modules:
  0.0 60.6 jit_solution(10825627206917604020)
XLA Ops:
  0.0 0.8 %select_reduce_fusion.1 = s32[256]{0:T(256)S(1)} fusion(s32[8]{0:T(128)} %param.9, s32[256]{0:T(256)S(1)} %and_select_fusion.2), kind=kLoop, calls=%fused_computation.45 | loop fusion | flops 5888 | bytes 2080 | tf_op jit(solution)/shard_map/reduce_sum | solution.py:15
  0.8 1.2 %copy.30 = bf16[256,1024]{0,1:T(8,128)(2,1)S(1)} copy(bf16[256,1024]{1,0:T(8,128)(2,1)} %param.6) | data formatting | bytes 1048576 | tf_op args[0]
  2.1 1.0 %copy.32 = bf16[256,2,4,128]{3,0,2,1:T(8,128)(2,1)} copy(bf16[256,2,4,128]{0,3,2,1:T(8,128)(2,1)S(1)} %bitcast.99) | data formatting | bytes 1048576
  3.1 17.6 %all_gather.6 = bf16[1024,256]{1,0:T(8,128)(2,1)S(1)} all-gather(bf16[256,256]{1,0:T(8,128)(2,1)} %param.7), channel_id=1, replica_groups=mesh['groups'=2,'ctx'=4,'head'=2,'rep'=2] {'ctx'}, dimensions={0}, use_global_device_ids=true | all-gather | bytes 655360 | tf_op jit(solution)/shard_map/all_gather | solution.py:69
  20.7 0.9 %reshape.66 = bf16[2,2,256,2,128]{4,3,2,1,0:T(2,128)(2,1)} reshape(bf16[1024,256]{1,0:T(8,128)(2,1)S(1)} %all_gather.6) | data formatting | bytes 1048576 | tf_op jit(solution)/shard_map/reshape | solution.py:75
  21.6 16.6 %all_gather.7 = bf16[1024,256]{1,0:T(8,128)(2,1)S(1)} all-gather(bf16[256,256]{1,0:T(8,128)(2,1)} %param.8), channel_id=1, replica_groups=mesh['groups'=2,'ctx'=4,'head'=2,'rep'=2] {'ctx'}, dimensions={0}, use_global_device_ids=true | all-gather | bytes 655360 | tf_op jit(solution)/shard_map/all_gather | solution.py:70
  38.2 0.9 %reshape.68 = bf16[2,2,256,2,128]{4,3,2,1,0:T(2,128)(2,1)} reshape(bf16[1024,256]{1,0:T(8,128)(2,1)S(1)} %all_gather.7) | data formatting | bytes 1048576 | tf_op jit(solution)/shard_map/reshape | solution.py:76
  39.3 20.2 %while.15 = (s32[]{:T(128)}, f32[256,2,4]{0,2,1:T(4,128)S(1)}, f32[256,2,4]{0,2,1:T(4,128)S(1)}, f32[256,2,4,128]{0,3,2,1:T(8,128)S(1)}, s32[2,2,256]{2,1,0:T(2,...) while((s32[]{:T(128)}, f32[256,2,4]{0,2,1:T(4,128)S(1)}, ...), condition=%wide.region_5.6_spmd.clone, body=%wide.region_2.5_spmd.clone.sunk | while | flops 549871616 | bytes 19995776 | solution.py:87
  39.3 1.4 %constant_dynamic-slice_fusion.3 = (bf16[1,2,256,2,128]{4,3,2,1,0:T(2,128)(2,1)S(1)}, bf16[1,2,256,2,128]{4,3,2,1,0:T(2,128)(2,1)S(1)}) fusion(bf16[2,2,256,2,128]{4,3,2,1,0:T(2,128)(2,1)} %get-tuple-element.251, s32[]{:T(128)} %get-tuple-element.232, bf16[2,2,256,2,128]{4,3,2,1,0:T(2,128)(2,1)} %get-tuple-element.249), kind=kLoop, calls=%fused_computation.38.clone.1 | loop fusion | bytes 1048580 | tf_op jit(solution)/shard_map/while/body/jit(dynamic_index_in_dim)/dynamic_slice | solution.py:87
  40.7 0.1 broadcast_compare_fusion.3
  40.8 1.9 %fusion.43 = (f32[2,256,2,4]{1,3,0,2:T(4,128)S(1)}, f32[2,2,256,256,4]{3,2,4,1,0:T(8,128)S(1)}) fusion(pred[2,256,256]{1,2,0:T(8,128)(4,1)S(1)} %broadcast_compare_fusion.3, bf16[256,2,4,128]{3,0,2,1:T(8,128)(2,1)} %get-tuple-element.250, bf16[1,2,256,2,128]{4,3,2,1,0:T(2,128)(2,1)S(1)} %get-tuple-element.209), kind=kOutput, calls=%fused_computation.2.clone.1 | convolution fusion | flops 271577088 | bytes 5128192 | tf_op jit(solution)/shard_map/while/body/eval_jaxpr/rhgd,cshd->crhgs/dot_general | solution.py:24
  42.7 1.2 %fusion.44 = (bf16[2,256,2,4,256]{1,4,3,0,2:T(8,128)(2,1)S(1)}, f32[2,256,2,4]{1,3,0,2:T(4,128)S(1)}) fusion(f32[2,2,256,256,4]{3,2,4,1,0:T(8,128)S(1)} %get-tuple-element.211, f32[2,256,2,4]{1,3,0,2:T(4,128)S(1)} %get-tuple-element.210, pred[2,256,256]{1,2,0:T(8,128)(4,1)S(1)} %broadcast_compare_fusion.3), kind=kLoop, calls=%fused_computation.3.clone.1 | loop fusion | flops 6287360 | bytes 6455296 | tf_op jit(solution)/shard_map/while/body/eval_jaxpr/convert_element_type | solution.py:34
  43.9 0.9 %copy.63 = bf16[1,2,256,2,128]{2,4,3,1,0:T(8,128)(2,1)} copy(bf16[1,2,256,2,128]{4,3,2,1,0:T(2,128)(2,1)S(1)} %get-tuple-element.216) | data formatting | bytes 524288 | tf_op jit(solution)/shard_map/while/body/jit(dynamic_index_in_dim)/dynamic_slice | solution.py:87
  44.8 2.4 %fusion.46 = bf16[2,256,2,4,128]{1,4,3,2,0:T(8,128)(2,1)} fusion(bf16[2,256,2,4,256]{1,4,3,0,2:T(8,128)(2,1)S(1)} %get-tuple-element.215, bf16[1,2,256,2,128]{2,4,3,1,0:T(8,128)(2,1)} %copy.63, f32[2,256,2,4]{1,3,0,2:T(4,128)S(1)} %get-tuple-element.212), kind=kOutput, calls=%fused_computation.6.clone.1 | convolution fusion | flops 269488128 | bytes 3424256 | tf_op jit(solution)/shard_map/while/body/eval_jaxpr/crhgs,cshd->crhgd/dot_general | solution.py:32
  47.2 2.1 %fusion.47 = f32[256,2,4,128]{0,3,2,1:T(8,128)S(1)} fusion(f32[256,2,4,128]{0,3,2,1:T(8,128)S(1)} %get-tuple-element.235, bf16[2,256,2,4,128]{1,4,3,2,0:T(8,128)(2,1)} %fusion.46, f32[256,2,4]{0,2,1:T(4,128)S(1)} %get-tuple-element.217, f32[256,2,4]{0,2,1:T(4,128)S(1)} %get-tuple-element.218, f32[256,2,4]{0,2,1:T(4,128)S(1)} %get-tuple-element.219, ...), kind=kLoop, calls=%fused_computation.10.clone.1 | loop fusion | flops 2359296 | bytes 3178497 | tf_op jit(solution)/shard_map/while/body/eval_jaxpr/add | solution.py:50
  49.4 1.4 %constant_dynamic-slice_fusion.3 = (bf16[1,2,256,2,128]{4,3,2,1,0:T(2,128)(2,1)S(1)}, bf16[1,2,256,2,128]{4,3,2,1,0:T(2,128)(2,1)S(1)}) fusion(bf16[2,2,256,2,128]{4,3,2,1,0:T(2,128)(2,1)} %get-tuple-element.251, s32[]{:T(128)} %get-tuple-element.232, bf16[2,2,256,2,128]{4,3,2,1,0:T(2,128)(2,1)} %get-tuple-element.249), kind=kLoop, calls=%fused_computation.38.clone.1 | loop fusion | bytes 1048580 | tf_op jit(solution)/shard_map/while/body/jit(dynamic_index_in_dim)/dynamic_slice | solution.py:87
  50.8 0.1 broadcast_compare_fusion.3
  50.9 1.9 %fusion.43 = (f32[2,256,2,4]{1,3,0,2:T(4,128)S(1)}, f32[2,2,256,256,4]{3,2,4,1,0:T(8,128)S(1)}) fusion(pred[2,256,256]{1,2,0:T(8,128)(4,1)S(1)} %broadcast_compare_fusion.3, bf16[256,2,4,128]{3,0,2,1:T(8,128)(2,1)} %get-tuple-element.250, bf16[1,2,256,2,128]{4,3,2,1,0:T(2,128)(2,1)S(1)} %get-tuple-element.209), kind=kOutput, calls=%fused_computation.2.clone.1 | convolution fusion | flops 271577088 | bytes 5128192 | tf_op jit(solution)/shard_map/while/body/eval_jaxpr/rhgd,cshd->crhgs/dot_general | solution.py:24
  52.8 1.2 %fusion.44 = (bf16[2,256,2,4,256]{1,4,3,0,2:T(8,128)(2,1)S(1)}, f32[2,256,2,4]{1,3,0,2:T(4,128)S(1)}) fusion(f32[2,2,256,256,4]{3,2,4,1,0:T(8,128)S(1)} %get-tuple-element.211, f32[2,256,2,4]{1,3,0,2:T(4,128)S(1)} %get-tuple-element.210, pred[2,256,256]{1,2,0:T(8,128)(4,1)S(1)} %broadcast_compare_fusion.3), kind=kLoop, calls=%fused_computation.3.clone.1 | loop fusion | flops 6287360 | bytes 6455296 | tf_op jit(solution)/shard_map/while/body/eval_jaxpr/convert_element_type | solution.py:34
  54.0 0.9 %copy.63 = bf16[1,2,256,2,128]{2,4,3,1,0:T(8,128)(2,1)} copy(bf16[1,2,256,2,128]{4,3,2,1,0:T(2,128)(2,1)S(1)} %get-tuple-element.216) | data formatting | bytes 524288 | tf_op jit(solution)/shard_map/while/body/jit(dynamic_index_in_dim)/dynamic_slice | solution.py:87
  54.9 2.4 %fusion.46 = bf16[2,256,2,4,128]{1,4,3,2,0:T(8,128)(2,1)} fusion(bf16[2,256,2,4,256]{1,4,3,0,2:T(8,128)(2,1)S(1)} %get-tuple-element.215, bf16[1,2,256,2,128]{2,4,3,1,0:T(8,128)(2,1)} %copy.63, f32[2,256,2,4]{1,3,0,2:T(4,128)S(1)} %get-tuple-element.212), kind=kOutput, calls=%fused_computation.6.clone.1 | convolution fusion | flops 269488128 | bytes 3424256 | tf_op jit(solution)/shard_map/while/body/eval_jaxpr/crhgs,cshd->crhgd/dot_general | solution.py:32
  57.3 2.1 %fusion.47 = f32[256,2,4,128]{0,3,2,1:T(8,128)S(1)} fusion(f32[256,2,4,128]{0,3,2,1:T(8,128)S(1)} %get-tuple-element.235, bf16[2,256,2,4,128]{1,4,3,2,0:T(8,128)(2,1)} %fusion.46, f32[256,2,4]{0,2,1:T(4,128)S(1)} %get-tuple-element.217, f32[256,2,4]{0,2,1:T(4,128)S(1)} %get-tuple-element.218, f32[256,2,4]{0,2,1:T(4,128)S(1)} %get-tuple-element.219, ...), kind=kLoop, calls=%fused_computation.10.clone.1 | loop fusion | flops 2359296 | bytes 3178497 | tf_op jit(solution)/shard_map/while/body/eval_jaxpr/add | solution.py:50
  59.5 0.1 divide_convert_fusion
  59.6 1.0 %copy.39 = bf16[256,1024]{1,0:T(8,128)(2,1)} copy(bf16[256,1024]{0,1:T(8,128)(2,1)S(1)} %bitcast.98) | data formatting | bytes 1048576 | tf_op jit(solution)/shard_map/convert_element_type | solution.py:89
  (16 shorter events, 0.2 us)
Async XLA Ops:
  0.0 39.1 %copy-start = (s32[8]{0:T(128)S(1)}, s32[8]{0:T(128)}, u32[]{:S(2)}) copy-start(s32[8]{0:T(128)} %param.9) | copy-start | bytes 100
where the time goes:
time: 61 us; the launch traced here: 60.6 us
  blocking collectives  34.1 us (56%)
  local copies, waits for them, and re-layouts  9.69 us (16%)
  matrix products  8.65 us (14%)
  other arithmetic  7.94 us (13%)
    all_gather x1, blocking collectives, shards(): k_piece = lax.all_gather(keys, 'ctx', axis=0, tiled=True)  17.6 us
    all_gather x1, blocking collectives, shards(): v_piece = lax.all_gather(values, 'ctx', axis=0, tiled=True)  16.6 us
    dot_general x2, matrix products, source_partials(): jnp.einsum('crhgs,cshd->crhgd', weights.astype(jnp.bfloat16), value_group...  4.85 us
    dynamic_slice x4, local copies, waits for them, and re-layouts, shards(): running, unused = lax.scan(one_turn, running, (k_steps, v_steps, p_steps))  4.53 us
    add x2, other arithmetic, absorb(): run_sum * rescale[..., None]  4.23 us
    dot_general x2, matrix products, source_partials(): jnp.einsum('rhgd,cshd->crhgs', query_block, key_group, preferred_element_...  3.8 us
    convert_element_type x2, other arithmetic, source_partials(): weights.astype(jnp.bfloat16)  2.34 us
    unnamed x4, local copies, waits for them, and re-layouts  2.27 us

commit v1 on v0

--- a/solution.py
+++ b/solution.py
@@ -66,8 +66,11 @@
         jnp.zeros((rows_here, kv_heads, common_values, head_dim), jnp.float32),
     )
     running = initial
-    k_piece = lax.all_gather(keys, "ctx", axis=0, tiled=True)
-    v_piece = lax.all_gather(values, "ctx", axis=0, tiled=True)
+    k_piece, v_piece = jnp.split(
+        jax.lax.all_gather(jnp.concatenate([keys, values], axis=1), "ctx", axis=0, tiled=True),
+        [keys.shape[1]],
+        axis=1,
+    )
     shard_count = k_piece.shape[0] // rows_here
     per_turn = 2
     turn_count = shard_count // per_turn

time: 61 us -> 71.3 us (1.17)
  blocking collectives: 34.1 us -> 0 us
  waiting for transfers between devices: 0 us -> 27.5 us
  between operations: 0.06 us -> 13.5 us
  other arithmetic: 7.94 us -> 10.2 us
  local copies, waits for them, and re-layouts: 9.69 us -> 10.9 us
    all_gather x2 -> x0, blocking collectives: 34.1 us -> none  [the longest x1 17.6 us: shards(): k_piece = lax.all_gather(keys, 'ctx', axis=0, tiled=True)]
    all_gather x0 -> x1, waiting for transfers between devices: none -> 27.5 us  [shards(): jax.lax.all_gather(jnp.concatenate([keys, values], axis=1), 'ctx', axis=0...]
    concatenate x0 -> x1, other arithmetic: none -> 1.69 us  [shards(): jnp.concatenate([keys, values], axis=1)]
    split x0 -> x1, local copies, waits for them, and re-layouts: none -> 1.27 us  [shards(): jnp.split(jax.lax.all_gather(jnp.concatenate([keys, values], axis=1), 'ct...]
    unnamed x4 -> x2, local copies, waits for them, and re-layouts: 2.27 us -> 2.27 us
  transfers between devices with their start and end apart: 0 -> 1, of which waited for: 0 -> 1; matrix products, arithmetic and copies ran while one was open for 0% -> 5% of each run, Pallas kernels for 0% -> 0%
where the time goes in v1:
time: 71.3 us; the launch traced here: 70.9 us
  waiting for transfers between devices  27.5 us (39%)
  between operations  13.5 us (19%)
  local copies, waits for them, and re-layouts  10.9 us (15%)
  other arithmetic  10.2 us (14%)
  matrix products  8.61 us (12%)
    all_gather x1, waiting for transfers between devices, shards(): jax.lax.all_gather(jnp.concatenate([keys, values], axis=1), 'ctx', axis=0...  27.5 us
    dot_general x2, matrix products, source_partials(): jnp.einsum('crhgs,cshd->crhgd', weights.astype(jnp.bfloat16), value_group...  4.85 us
    dynamic_slice x4, local copies, waits for them, and re-layouts, shards(): running, unused = lax.scan(one_turn, running, (k_steps, v_steps, p_steps))  4.53 us
    add x2, other arithmetic, absorb(): run_sum * rescale[..., None]  4.23 us
    dot_general x2, matrix products, source_partials(): jnp.einsum('rhgd,cshd->crhgs', query_block, key_group, preferred_element_...  3.77 us
    convert_element_type x2, other arithmetic, source_partials(): weights.astype(jnp.bfloat16)  2.34 us
    unnamed x2, local copies, waits for them, and re-layouts  2.27 us
    concatenate x1, other arithmetic, shards(): jnp.concatenate([keys, values], axis=1)  1.69 us
  transfers between devices with their start and end apart: 1, of which 1 were waited for; matrix products, arithmetic and copies ran while one was open for 5% of the time, Pallas kernels for 0%

profile of v1, /device:TPU:0, one launch (start us, length us, event | category | flops | bytes accessed | tf_op | source)
XLA Modules:
  0.0 70.9 jit_solution(11305848871449782462)
XLA Ops:
  6.5 1.7 %pad_maximum_fusion = bf16[256,512]{1,0:T(8,128)(2,1)} fusion(bf16[256,256]{1,0:T(8,128)(2,1)} %param.8, bf16[256,256]{1,0:T(8,128)(2,1)} %param.7), kind=kLoop, calls=%fused_computation.41 | loop fusion | flops 524288 | bytes 524288 | tf_op jit(solution)/shard_map/concatenate | solution.py:70
  8.3 1.2 %copy.30 = bf16[256,1024]{0,1:T(8,128)(2,1)S(1)} copy(bf16[256,1024]{1,0:T(8,128)(2,1)} %param.6) | data formatting | bytes 1048576 | tf_op args[0]
  9.5 1.0 %copy.32 = bf16[256,2,4,128]{3,0,2,1:T(8,128)(2,1)} copy(bf16[256,2,4,128]{0,3,2,1:T(8,128)(2,1)S(1)} %bitcast.99) | data formatting | bytes 1048576
  10.6 0.7 %select_reduce_fusion = s32[1024]{0:T(1024)S(1)} fusion(s32[8]{0:T(128)} %param.9, s32[1024]{0:T(1024)S(1)} %add_select_fusion), kind=kLoop, calls=%fused_computation.42 | loop fusion | flops 23552 | bytes 8224 | tf_op jit(solution)/shard_map/reduce_sum | solution.py:15
  11.3 0.7 %select_reduce_fusion.1 = s32[256]{0:T(256)S(1)} fusion(s32[8]{0:T(128)} %param.9, s32[256]{0:T(256)S(1)} %and_select_fusion.2), kind=kLoop, calls=%fused_computation.46 | loop fusion | flops 5888 | bytes 2080 | tf_op jit(solution)/shard_map/reduce_sum | solution.py:15
  12.1 27.5 %all-gather.2.cloned.1.call-done = bf16[1024,512]{1,0:T(8,128)(2,1)} async-done(((bf16[256,512]{1,0:T(8,128)(2,1)}), bf16[1024,512]{1,0:T(8,128)(2,1)}) %all-gather.2.cloned.1.call-update) | async-done | bytes 1048592 | tf_op jit(solution)/shard_map/all_gather | solution.py:70
  39.6 1.3 %fusion.31 = (bf16[1024,256]{1,0:T(8,128)(2,1)S(1)}, bf16[1024,256]{1,0:T(8,128)(2,1)S(1)}) fusion(bf16[1024,512]{1,0:T(8,128)(2,1)} %all-gather.2.cloned.1.call-done), kind=kLoop, calls=%fused_computation.68 | loop fusion | bytes 2097152 | tf_op jit(solution)/shard_map/split | solution.py:69
  40.9 0.9 %reshape.66 = bf16[2,2,256,2,128]{4,3,2,1,0:T(2,128)(2,1)} reshape(bf16[1024,256]{1,0:T(8,128)(2,1)S(1)} %get-tuple-element.143) | data formatting | bytes 1048576 | tf_op jit(solution)/shard_map/reshape | solution.py:78
  41.8 0.9 %reshape.68 = bf16[2,2,256,2,128]{4,3,2,1,0:T(2,128)(2,1)} reshape(bf16[1024,256]{1,0:T(8,128)(2,1)S(1)} %get-tuple-element.142) | data formatting | bytes 1048576 | tf_op jit(solution)/shard_map/reshape | solution.py:79
  42.8 20.1 %while.15 = (s32[]{:T(128)}, f32[256,2,4]{0,2,1:T(4,128)S(1)}, f32[256,2,4]{0,2,1:T(4,128)S(1)}, f32[256,2,4,128]{0,3,2,1:T(8,128)S(1)}, s32[2,2,256]{2,1,0:T(2,...) while((s32[]{:T(128)}, f32[256,2,4]{0,2,1:T(4,128)S(1)}, ...), condition=%wide.region_5.6_spmd.clone, body=%wide.region_2.5_spmd.clone.sunk | while | flops 549871616 | bytes 19995776 | solution.py:90
  42.8 1.4 %constant_dynamic-slice_fusion.3 = (bf16[1,2,256,2,128]{4,3,2,1,0:T(2,128)(2,1)S(1)}, bf16[1,2,256,2,128]{4,3,2,1,0:T(2,128)(2,1)S(1)}) fusion(bf16[2,2,256,2,128]{4,3,2,1,0:T(2,128)(2,1)} %get-tuple-element.253, s32[]{:T(128)} %get-tuple-element.234, bf16[2,2,256,2,128]{4,3,2,1,0:T(2,128)(2,1)} %get-tuple-element.251), kind=kLoop, calls=%fused_computation.38.clone.1 | loop fusion | bytes 1048580 | tf_op jit(solution)/shard_map/while/body/jit(dynamic_index_in_dim)/dynamic_slice | solution.py:90
  44.2 0.1 broadcast_compare_fusion.3
  44.3 1.9 %fusion.44 = (f32[2,256,2,4]{1,3,0,2:T(4,128)S(1)}, f32[2,2,256,256,4]{3,2,4,1,0:T(8,128)S(1)}) fusion(pred[2,256,256]{1,2,0:T(8,128)(4,1)S(1)} %broadcast_compare_fusion.3, bf16[256,2,4,128]{3,0,2,1:T(8,128)(2,1)} %get-tuple-element.252, bf16[1,2,256,2,128]{4,3,2,1,0:T(2,128)(2,1)S(1)} %get-tuple-element.211), kind=kOutput, calls=%fused_computation.2.clone.1 | convolution fusion | flops 271577088 | bytes 5128192 | tf_op jit(solution)/shard_map/while/body/eval_jaxpr/rhgd,cshd->crhgs/dot_general | solution.py:24
  46.2 1.2 %fusion.45 = (bf16[2,256,2,4,256]{1,4,3,0,2:T(8,128)(2,1)S(1)}, f32[2,256,2,4]{1,3,0,2:T(4,128)S(1)}) fusion(f32[2,2,256,256,4]{3,2,4,1,0:T(8,128)S(1)} %get-tuple-element.213, f32[2,256,2,4]{1,3,0,2:T(4,128)S(1)} %get-tuple-element.212, pred[2,256,256]{1,2,0:T(8,128)(4,1)S(1)} %broadcast_compare_fusion.3), kind=kLoop, calls=%fused_computation.3.clone.1 | loop fusion | flops 6287360 | bytes 6455296 | tf_op jit(solution)/shard_map/while/body/eval_jaxpr/convert_element_type | solution.py:34
  47.4 0.9 %copy.63 = bf16[1,2,256,2,128]{2,4,3,1,0:T(8,128)(2,1)} copy(bf16[1,2,256,2,128]{4,3,2,1,0:T(2,128)(2,1)S(1)} %get-tuple-element.218) | data formatting | bytes 524288 | tf_op jit(solution)/shard_map/while/body/jit(dynamic_index_in_dim)/dynamic_slice | solution.py:90
  48.3 2.4 %fusion.47 = bf16[2,256,2,4,128]{1,4,3,2,0:T(8,128)(2,1)} fusion(bf16[2,256,2,4,256]{1,4,3,0,2:T(8,128)(2,1)S(1)} %get-tuple-element.217, bf16[1,2,256,2,128]{2,4,3,1,0:T(8,128)(2,1)} %copy.63, f32[2,256,2,4]{1,3,0,2:T(4,128)S(1)} %get-tuple-element.214), kind=kOutput, calls=%fused_computation.6.clone.1 | convolution fusion | flops 269488128 | bytes 3424256 | tf_op jit(solution)/shard_map/while/body/eval_jaxpr/crhgs,cshd->crhgd/dot_general | solution.py:32
  50.7 2.1 %fusion.48 = f32[256,2,4,128]{0,3,2,1:T(8,128)S(1)} fusion(f32[256,2,4,128]{0,3,2,1:T(8,128)S(1)} %get-tuple-element.237, bf16[2,256,2,4,128]{1,4,3,2,0:T(8,128)(2,1)} %fusion.47, f32[256,2,4]{0,2,1:T(4,128)S(1)} %get-tuple-element.219, f32[256,2,4]{0,2,1:T(4,128)S(1)} %get-tuple-element.220, f32[256,2,4]{0,2,1:T(4,128)S(1)} %get-tuple-element.221, ...), kind=kLoop, calls=%fused_computation.10.clone.1 | loop fusion | flops 2359296 | bytes 3178497 | tf_op jit(solution)/shard_map/while/body/eval_jaxpr/add | solution.py:50
  52.8 1.4 %constant_dynamic-slice_fusion.3 = (bf16[1,2,256,2,128]{4,3,2,1,0:T(2,128)(2,1)S(1)}, bf16[1,2,256,2,128]{4,3,2,1,0:T(2,128)(2,1)S(1)}) fusion(bf16[2,2,256,2,128]{4,3,2,1,0:T(2,128)(2,1)} %get-tuple-element.253, s32[]{:T(128)} %get-tuple-element.234, bf16[2,2,256,2,128]{4,3,2,1,0:T(2,128)(2,1)} %get-tuple-element.251), kind=kLoop, calls=%fused_computation.38.clone.1 | loop fusion | bytes 1048580 | tf_op jit(solution)/shard_map/while/body/jit(dynamic_index_in_dim)/dynamic_slice | solution.py:90
  54.4 1.9 %fusion.44 = (f32[2,256,2,4]{1,3,0,2:T(4,128)S(1)}, f32[2,2,256,256,4]{3,2,4,1,0:T(8,128)S(1)}) fusion(pred[2,256,256]{1,2,0:T(8,128)(4,1)S(1)} %broadcast_compare_fusion.3, bf16[256,2,4,128]{3,0,2,1:T(8,128)(2,1)} %get-tuple-element.252, bf16[1,2,256,2,128]{4,3,2,1,0:T(2,128)(2,1)S(1)} %get-tuple-element.211), kind=kOutput, calls=%fused_computation.2.clone.1 | convolution fusion | flops 271577088 | bytes 5128192 | tf_op jit(solution)/shard_map/while/body/eval_jaxpr/rhgd,cshd->crhgs/dot_general | solution.py:24
  56.3 1.2 %fusion.45 = (bf16[2,256,2,4,256]{1,4,3,0,2:T(8,128)(2,1)S(1)}, f32[2,256,2,4]{1,3,0,2:T(4,128)S(1)}) fusion(f32[2,2,256,256,4]{3,2,4,1,0:T(8,128)S(1)} %get-tuple-element.213, f32[2,256,2,4]{1,3,0,2:T(4,128)S(1)} %get-tuple-element.212, pred[2,256,256]{1,2,0:T(8,128)(4,1)S(1)} %broadcast_compare_fusion.3), kind=kLoop, calls=%fused_computation.3.clone.1 | loop fusion | flops 6287360 | bytes 6455296 | tf_op jit(solution)/shard_map/while/body/eval_jaxpr/convert_element_type | solution.py:34
  57.5 0.9 %copy.63 = bf16[1,2,256,2,128]{2,4,3,1,0:T(8,128)(2,1)} copy(bf16[1,2,256,2,128]{4,3,2,1,0:T(2,128)(2,1)S(1)} %get-tuple-element.218) | data formatting | bytes 524288 | tf_op jit(solution)/shard_map/while/body/jit(dynamic_index_in_dim)/dynamic_slice | solution.py:90
  58.3 2.4 %fusion.47 = bf16[2,256,2,4,128]{1,4,3,2,0:T(8,128)(2,1)} fusion(bf16[2,256,2,4,256]{1,4,3,0,2:T(8,128)(2,1)S(1)} %get-tuple-element.217, bf16[1,2,256,2,128]{2,4,3,1,0:T(8,128)(2,1)} %copy.63, f32[2,256,2,4]{1,3,0,2:T(4,128)S(1)} %get-tuple-element.214), kind=kOutput, calls=%fused_computation.6.clone.1 | convolution fusion | flops 269488128 | bytes 3424256 | tf_op jit(solution)/shard_map/while/body/eval_jaxpr/crhgs,cshd->crhgd/dot_general | solution.py:32
  60.8 2.1 %fusion.48 = f32[256,2,4,128]{0,3,2,1:T(8,128)S(1)} fusion(f32[256,2,4,128]{0,3,2,1:T(8,128)S(1)} %get-tuple-element.237, bf16[2,256,2,4,128]{1,4,3,2,0:T(8,128)(2,1)} %fusion.47, f32[256,2,4]{0,2,1:T(4,128)S(1)} %get-tuple-element.219, f32[256,2,4]{0,2,1:T(4,128)S(1)} %get-tuple-element.220, f32[256,2,4]{0,2,1:T(4,128)S(1)} %get-tuple-element.221, ...), kind=kLoop, calls=%fused_computation.10.clone.1 | loop fusion | flops 2359296 | bytes 3178497 | tf_op jit(solution)/shard_map/while/body/eval_jaxpr/add | solution.py:50
  63.0 1.0 %copy.39 = bf16[256,1024]{1,0:T(8,128)(2,1)} copy(bf16[256,1024]{0,1:T(8,128)(2,1)S(1)} %bitcast.98) | data formatting | bytes 1048576 | tf_op jit(solution)/shard_map/convert_element_type | solution.py:92
  (17 shorter events, 0.4 us)
Async XLA Ops:
  6.5 33.1 %all-gather.2.cloned.1.call-start = ((), (), s32[]{:S(2)}) async-start(), calls=%async_computation | async-start | bytes 1310720 | tf_op jit(solution)/shard_map/all_gather | solution.py:70
Sparse Core Ops, SparseCore 0:
  8.9 30.6 all-gather.1
